TPU v7x, 1024 devices: a whole 4x4x32 slice. The times are simulated.
1024 devices in a mesh: grp: 16 (over y_hi, x, core), dp: 64 (over z, y_lo).
Axes of the slice: x: 4, y: 4 (y_hi: 2, y_lo: 2; y = y_hi * 2 + y_lo), z: 32, core: 2. Of those that a mesh axis runs over, the one named last changes fastest.
Arguments:
- query: bfloat16 [64, 2048, 2560], P('dp', 'grp'), may hold values from -30 to 30
- resp_kv: bfloat16 [64, 2048, 1024], P('dp', 'grp'), may hold values from -6 to 6
- prefix_kv: bfloat16 [64, 256, 1024], P('dp', 'grp'), may hold values from -30 to 30
- query_bias: float32 [2560], replicated, may hold values from -3 to 3
- kv_bias: float32 [1024], replicated, may hold values from -3 to 3
- out_grad: bfloat16 [64, 2048, 2560], P('dp', 'grp'), may hold values from -6 to 6
- lengths: int32 [64, 16], P('dp', 'grp'), may hold values from 32 to 128
Outputs:
- attended: bfloat16 [64, 2048, 2560], P('dp', 'grp')
- query_grad: bfloat16 [64, 2048, 2560], P('dp', 'grp')
- resp_kv_grad: bfloat16 [64, 2048, 1024], P('dp', 'grp')
- prefix_kv_grad: bfloat16 [64, 256, 1024], P('dp', 'grp')
- query_bias_grad: float32 [2560], replicated
- kv_bias_grad: float32 [1024], replicated
All inputs are finite; a program needn't handle non-finite values.
Results may differ from a plain program's by a relative error of at most 0.013.
The roundings to bfloat16 on the way count: a program that leaves them out, or rounds other values in their place, can miss the bound.
Values may be sent and summed in bfloat16 or wider, within the bound.
No kernel may reach another device: no remote copies, remote signals or barrier semaphores. Data moves between devices by JAX's collectives and lax.ppermute only.
A program may use at most 32 MiB of HBM per device.

v0:
```python
import functools

import jax
import jax.numpy as jnp
from jax import lax
from jax.sharding import Mesh
from jax.sharding import PartitionSpec as P

QH = 20
KVH = 4
HD = 128
GRP = ("grp_0", "grp_1", "grp_2")
GRP_DP = ("grp_0", "grp_1", "grp_2", "dp_0", "dp_1")
DP = ("dp_0", "dp_1")


NEG_BIG = -1e30


def copy_for_each(shard, axis):
    copies = jnp.broadcast_to(shard, (lax.axis_size(axis), *shard.shape))
    return lax.all_to_all(copies, axis, split_axis=0, concat_axis=0, tiled=True)


def in_order(pieces, dim):
    pieces = jnp.moveaxis(pieces, 0, dim)
    dims = pieces.shape
    return pieces.reshape(*dims[:dim], dims[dim] * dims[dim + 1], *dims[dim + 2 :])


def gathered_copies(shard, axis, dim):
    pieces = copy_for_each(shard, axis)
    return in_order(pieces, dim)


def cut_along(shard, dim, count):
    before, after = (shard.shape[:dim], shard.shape[dim + 1 :])
    return jnp.moveaxis(shard.reshape(*before, count, -1, *after), dim, 0)


def summed_on_arrival(shard, axis, dim):
    count = lax.axis_size(axis)
    pieces = lax.all_to_all(cut_along(shard, dim, count), axis, 0, 0, tiled=True)
    return jnp.sum(pieces.astype(jnp.float32), axis=0)


def by_axis(shard, axes):
    return functools.reduce(lax.psum, axes, shard)


def attend_group(queries, cotangent, key_blocks, value_blocks, allows):
    factor = queries.shape[-1] ** (-0.5)
    scores = []
    for keys, allow in zip(key_blocks, allows):
        raw = jnp.einsum("thd,sd->hts", queries, keys, preferred_element_type=jnp.float32) * factor
        scores.append(jnp.where(allow[None], raw, NEG_BIG))
    highest = jnp.max(scores[0], -1, keepdims=True)
    for item in scores[1:]:
        highest = jnp.maximum(highest, jnp.max(item, -1, keepdims=True))
    powers = [jnp.exp(item - highest) for item in scores]
    totals = sum((jnp.sum(item, -1, keepdims=True) for item in powers))
    chances = [item / totals for item in powers]
    rounded = [item.astype(jnp.bfloat16) for item in chances]
    output = sum(
        (
            jnp.einsum("hts,sd->thd", wts, vals, preferred_element_type=jnp.float32)
            for wts, vals in zip(rounded, value_blocks)
        )
    )
    slopes = [
        jnp.einsum("thd,sd->hts", cotangent, vals, preferred_element_type=jnp.float32)
        for vals in value_blocks
    ]
    row_dot = sum(
        (jnp.sum(prob * slope, -1, keepdims=True) for prob, slope in zip(chances, slopes))
    )
    shifted = [
        (prob * (slope - row_dot)).astype(jnp.bfloat16) for prob, slope in zip(chances, slopes)
    ]
    query_grad = (
        sum(
            (
                jnp.einsum("hts,sd->thd", dsb, keys, preferred_element_type=jnp.float32)
                for dsb, keys in zip(shifted, key_blocks)
            )
        )
        * factor
    )
    key_grads = [
        jnp.einsum("hts,thd->sd", dsb, queries, preferred_element_type=jnp.float32) * factor
        for dsb in shifted
    ]
    value_grads = [
        jnp.einsum("hts,thd->sd", wts, cotangent, preferred_element_type=jnp.float32)
        for wts in rounded
    ]
    return (output, query_grad, key_grads, value_grads, shifted, rounded)


def local(query, resp_kv, prefix_kv, query_bias, kv_bias, out_grad, lengths):
    group = QH // KVH
    width = KVH * HD
    factor = HD ** (-0.5)
    prefix_own = (prefix_kv[0].astype(jnp.float32) + kv_bias).astype(jnp.bfloat16)
    own_rows = prefix_own.shape[0]
    prefix = gathered_copies(prefix_own, GRP, 0)
    slots = query.shape[1]
    pre_rows = prefix.shape[0]
    length = lengths[0, 0]
    biased_query = (query[0].astype(jnp.float32) + query_bias).astype(jnp.bfloat16)
    own_kv = (resp_kv[0].astype(jnp.float32) + kv_bias).astype(jnp.bfloat16)
    position = jnp.arange(slots, dtype=jnp.int32)
    live = position < length
    grad_live = jnp.where(live[:, None], out_grad[0], jnp.zeros_like(out_grad[0]))
    allow_own = position[None, :] <= position[:, None]
    allow_pre = jnp.ones((slots, pre_rows), dtype=bool)
    queries = biased_query.reshape(slots, KVH, group, HD).transpose(1, 0, 2, 3)
    grads = grad_live.reshape(slots, KVH, group, HD).transpose(1, 0, 2, 3)
    pre_keys = prefix[:, :width].reshape(pre_rows, KVH, HD).transpose(1, 0, 2)
    pre_vals = prefix[:, width:].reshape(pre_rows, KVH, HD).transpose(1, 0, 2)
    own_keys = own_kv[:, :width].reshape(slots, KVH, HD).transpose(1, 0, 2)
    own_vals = own_kv[:, width:].reshape(slots, KVH, HD).transpose(1, 0, 2)

    def per_group(pieces):
        qpart, gpart, pkey, pval, okey, oval = pieces
        output, qgrad, kgrads, vgrads, shifted, rounded = attend_group(
            qpart, gpart, [okey, pkey], [oval, pval], [allow_own, allow_pre]
        )
        return (output, qgrad, kgrads[1], vgrads[1], kgrads[0], vgrads[0], shifted[1], rounded[1])

    output, qgrad, pk_grad, pv_grad, ok_grad, ov_grad, pre_shift, pre_prob = lax.map(
        per_group, (queries, grads, pre_keys, pre_vals, own_keys, own_vals)
    )
    output = output.transpose(1, 0, 2, 3).reshape(slots, QH * HD)
    attended = jnp.where(live[:, None], output, 0.0).astype(jnp.bfloat16)
    qgrad = qgrad.transpose(1, 0, 2, 3).reshape(slots, QH * HD)
    own_grad = jnp.concatenate(
        [
            ok_grad.transpose(1, 0, 2).reshape(slots, width),
            ov_grad.transpose(1, 0, 2).reshape(slots, width),
        ],
        -1,
    )
    shift_sum = jnp.sum(pre_shift.astype(jnp.float32), -1)
    prob_sum = jnp.sum(pre_prob.astype(jnp.float32), -1)
    key_total = jnp.einsum("jht,jthd->jd", shift_sum, queries.astype(jnp.float32)) * factor
    value_total = jnp.einsum("jht,jthd->jd", prob_sum, grads.astype(jnp.float32))
    pre_total = jnp.concatenate([key_total.reshape(width), value_total.reshape(width)], -1)
    count = own_rows * lax.axis_size(GRP)
    shift_part = lax.slice_in_dim(pre_shift, 0, count, axis=3)
    prob_part = lax.slice_in_dim(pre_prob, 0, count, axis=3)
    key_part = (
        jnp.einsum("jhts,jthd->sjd", shift_part, queries, preferred_element_type=jnp.float32)
        * factor
    )
    value_part = jnp.einsum("jhts,jthd->sjd", prob_part, grads, preferred_element_type=jnp.float32)
    prefix_grad = summed_on_arrival(
        jnp.concatenate(
            [key_part.reshape(count, width), value_part.reshape(count, width)], -1
        ).astype(jnp.bfloat16),
        GRP,
        0,
    ).astype(jnp.bfloat16)
    qsum, kvsum = (
        by_axis(jnp.sum(qgrad, 0), GRP_DP),
        by_axis(jnp.sum(own_grad, 0) + pre_total, GRP_DP),
    )
    return (
        attended[None],
        qgrad.astype(jnp.bfloat16)[None],
        own_grad.astype(jnp.bfloat16)[None],
        prefix_grad[None],
        qsum,
        kvsum,
    )


def solution(mesh):
    finer = Mesh(mesh.devices.reshape(2, 4, 2, 32, 2), ("grp_0", "grp_1", "grp_2", "dp_0", "dp_1"))
    in_specs = (
        P(DP, GRP, None),
        P(DP, GRP, None),
        P(DP, GRP, None),
        P(),
        P(),
        P(DP, GRP, None),
        P(DP, GRP),
    )
    out_specs = (P(DP, GRP, None), P(DP, GRP, None), P(DP, GRP, None), P(DP, GRP, None), P(), P())
    return jax.shard_map(local, mesh=finer, in_specs=in_specs, out_specs=out_specs, check_vma=False)
```

profile of v0, /device:TPU:8, one launch (start us, length us, event | category | flops | bytes accessed | tf_op | source)
XLA Modules:
  0.0 233.5 jit_solution(958982717674805713)
XLA Ops:
  2.3 6.1 %all-to-all-start = ((bf16[16,16,1024]{2,1,0:T(8,128)(2,1)}), bf16[16,16,1024]{2,1,0:T(8,128)(2,1)S(1)}, u32[]{:S(2)}, u32[]{:S(2)}) async-start(bf16[16,16,1024]{2,1,0:T(8,128)(2,1)} %broadcast_in_dim.88), calls=%async_computation | async-start | bytes 1048576 | tf_op jit(solution)/shard_map/all_to_all | solution.py:22
  10.9 9.9 %all-to-all-done = bf16[16,16,1024]{2,1,0:T(8,128)(2,1)S(1)} async-done(((bf16[16,16,1024]{2,1,0:T(8,128)(2,1)}), bf16[16,16,1024]{2,1,0:T(8,128)(2,1)S(1)}, u32[]{:S(2)}, u32[]{:S(2)}) %all-to-all-start) | async-done | bytes 524320 | tf_op jit(solution)/shard_map/all_to_all | solution.py:22
  21.1 26.6 %while.21 = (s32[]{:T(128)}, bf16[4,128,5,128]{1,3,2,0:T(8,128)(2,1)}, f32[4,128,5,128]{1,3,2,0:T(8,128)}, f32[4,128,128]{1,2,0:T(8,128)}, f32[4,128,128]{1,2,0:...) while((s32[]{:T(128)}, ...), condition=%wide.region_7.8_spmd.clone, body=%wide.region_0.7_spmd.clone.sunk | while | flops 298301568 | bytes 14983897 | solution.py:131
  25.8 1.1 bitcast_dynamic-update-slice_fusion.3
  32.4 1.1 bitcast_dynamic-update-slice_fusion.3
  39.0 1.1 bitcast_dynamic-update-slice_fusion.3
  45.7 1.1 bitcast_dynamic-update-slice_fusion.3
  47.8 2.0 fusion.67
  49.7 1.8 convert_reduce_fusion
  51.6 1.3 fusion.68
  52.8 1.3 select_convert_fusion
  54.2 1.1 copy.56
  55.4 1.8 copy.55
  57.2 1.7 concatenate.33
  59.8 1.8 concatenate.32
  63.7 3.6 %all-to-all-start.1 = ((bf16[16,16,1024]{2,1,0:T(8,128)(2,1)}), bf16[16,16,1024]{2,1,0:T(8,128)(2,1)S(1)}, u32[]{:S(2)}, u32[]{:S(2)}) async-start(bf16[16,16,1024]{2,1,0:T(8,128)(2,1)} %pad_maximum_fusion), calls=%async_computation.1 | async-start | bytes 1048576 | tf_op jit(solution)/shard_map/all_to_all | solution.py:43
  67.3 1.0 bitcast_convert_fusion.1
  68.7 1.1 copy.57
  70.0 1.2 maximum_reduce_fusion
  71.2 11.4 %all-reduce.4 = (f32[2560]{0:T(1024)S(1)}, f32[1024]{0:T(1024)S(1)}) all-reduce(f32[2560]{0:T(1024)S(1)} %reduce_sum.88, f32[1024]{0:T(1024)S(1)} %maximum_add_fusion), channel_id=1, replica_groups=mesh['grp_0'=2,'grp_1'=4,'grp_2'=2,'dp_0'=32,'dp_1'=2] {'grp_0'}, use_global_device_ids=true, to_apply=%region_10.11 | all-reduce | flops 3584 | bytes 28672 | tf_op jit(solution)/shard_map/psum | solution.py:48
  82.7 16.9 %all-reduce.1 = (f32[2560]{0:T(1024)S(1)}, f32[1024]{0:T(1024)S(1)}) all-reduce(f32[2560]{0:T(1024)S(1)} %get-tuple-element.170, f32[1024]{0:T(1024)S(1)} %get-tuple-element.171), channel_id=1, replica_groups=mesh['grp_0'=2,'grp_1'=4,'grp_2'=2,'dp_0'=32,'dp_1'=2] {'grp_1'}, use_global_device_ids=true, to_apply=%region_11.12 | all-reduce | flops 3584 | bytes 28672 | tf_op jit(solution)/shard_map/psum | solution.py:48
  99.5 3.3 %all-reduce.3 = (f32[2560]{0:T(1024)S(1)}, f32[1024]{0:T(1024)S(1)}) all-reduce(f32[2560]{0:T(1024)S(1)} %get-tuple-element.164, f32[1024]{0:T(1024)S(1)} %get-tuple-element.165), channel_id=1, replica_groups=mesh['grp_0'=2,'grp_1'=4,'grp_2'=2,'dp_0'=32,'dp_1'=2] {'grp_2'}, use_global_device_ids=true, to_apply=%region_12.13 | all-reduce | flops 3584 | bytes 28672 | tf_op jit(solution)/shard_map/psum | solution.py:48
  102.8 120.7 %all-reduce = (f32[2560]{0:T(1024)S(1)}, f32[1024]{0:T(1024)S(1)}) all-reduce(f32[2560]{0:T(1024)S(1)} %get-tuple-element.168, f32[1024]{0:T(1024)S(1)} %get-tuple-element.169), channel_id=1, replica_groups=mesh['grp_0'=2,'grp_1'=4,'grp_2'=2,'dp_0'=32,'dp_1'=2] {'dp_0'}, use_global_device_ids=true, to_apply=%region_13.14 | all-reduce | flops 3584 | bytes 28672 | tf_op jit(solution)/shard_map/psum | solution.py:48
  223.5 8.5 %all-reduce.2 = (f32[2560]{0:T(1024)}, f32[1024]{0:T(1024)}) all-reduce(f32[2560]{0:T(1024)S(1)} %get-tuple-element.162, f32[1024]{0:T(1024)S(1)} %get-tuple-element.163), channel_id=1, replica_groups=mesh['grp_0'=2,'grp_1'=4,'grp_2'=2,'dp_0'=32,'dp_1'=2] {'dp_1'}, use_global_device_ids=true, to_apply=%region_14.15 | all-reduce | flops 3584 | bytes 28672 | tf_op jit(solution)/shard_map/psum | solution.py:48
  (152 shorter events, 30.4 us)
Async XLA Ops:
  0.6 8.9 %copy-start.10 = (f32[1024]{0:T(1024)S(1)}, f32[1024]{0:T(1024)}, u32[]{:S(2)}) copy-start(f32[1024]{0:T(1024)} %param.13) | copy-start | bytes 12292
  0.6 8.6 %copy-start.11 = (f32[2560]{0:T(1024)S(1)}, f32[2560]{0:T(1024)}, u32[]{:S(2)}) copy-start(f32[2560]{0:T(1024)} %param.12) | copy-start | bytes 30724
  0.7 8.7 %copy-start.7 = (bf16[1,128,1024]{2,1,0:T(8,128)(2,1)S(1)}, bf16[1,128,1024]{2,1,0:T(8,128)(2,1)}, u32[]{:S(2)}) copy-start(bf16[1,128,1024]{2,1,0:T(8,128)(2,1)} %param.10) | copy-start | bytes 786436
  1.5 8.2 %copy-start.5 = (bf16[1,128,2560]{2,1,0:T(8,128)(2,1)S(1)}, bf16[1,128,2560]{2,1,0:T(8,128)(2,1)}, u32[]{:S(2)}) copy-start(bf16[1,128,2560]{2,1,0:T(8,128)(2,1)} %param.9) | copy-start | bytes 1966084
  2.3 18.5 %all-to-all-start = ((bf16[16,16,1024]{2,1,0:T(8,128)(2,1)}), bf16[16,16,1024]{2,1,0:T(8,128)(2,1)S(1)}, u32[]{:S(2)}, u32[]{:S(2)}) async-start(bf16[16,16,1024]{2,1,0:T(8,128)(2,1)} %broadcast_in_dim.88), calls=%async_computation | async-start | bytes 1048576 | tf_op jit(solution)/shard_map/all_to_all | solution.py:22
  8.5 1.6 copy-start.6
  9.3 1.1 copy-start.13
  21.2 3.0 %copy-start.8 = (bf16[4,256,128]{1,2,0:T(8,128)(2,1)}, bf16[4,256,128]{1,2,0:T(8,128)(2,1)S(1)}, u32[]{:S(2)}) copy-start(bf16[4,256,128]{1,2,0:T(8,128)(2,1)S(1)} %get-tuple-element.331) | copy-start | bytes 786436 | tf_op jit(solution)/shard_map/while
  25.8 2.0 copy-start.9
  27.8 3.0 %copy-start.8 = (bf16[4,256,128]{1,2,0:T(8,128)(2,1)}, bf16[4,256,128]{1,2,0:T(8,128)(2,1)S(1)}, u32[]{:S(2)}) copy-start(bf16[4,256,128]{1,2,0:T(8,128)(2,1)S(1)} %get-tuple-element.331) | copy-start | bytes 786436 | tf_op jit(solution)/shard_map/while
  32.4 2.1 copy-start.9
  34.4 3.0 %copy-start.8 = (bf16[4,256,128]{1,2,0:T(8,128)(2,1)}, bf16[4,256,128]{1,2,0:T(8,128)(2,1)S(1)}, u32[]{:S(2)}) copy-start(bf16[4,256,128]{1,2,0:T(8,128)(2,1)S(1)} %get-tuple-element.331) | copy-start | bytes 786436 | tf_op jit(solution)/shard_map/while
  39.0 2.1 copy-start.9
  41.1 3.0 %copy-start.8 = (bf16[4,256,128]{1,2,0:T(8,128)(2,1)}, bf16[4,256,128]{1,2,0:T(8,128)(2,1)S(1)}, u32[]{:S(2)}) copy-start(bf16[4,256,128]{1,2,0:T(8,128)(2,1)S(1)} %get-tuple-element.331) | copy-start | bytes 786436 | tf_op jit(solution)/shard_map/while
  45.7 2.1 copy-start.9
  47.8 2.0 copy-start
  51.6 1.3 copy-start.14
  52.8 2.4 %copy-start.1 = (f32[4,128,5,128]{1,3,2,0:T(8,128)S(1)}, f32[4,128,5,128]{1,3,2,0:T(8,128)}, u32[]{:S(2)}) copy-start(f32[4,128,5,128]{1,3,2,0:T(8,128)} %get-tuple-element.84) | copy-start | bytes 3932164
  59.8 3.0 %copy-start.3 = (bf16[16,16,512]{2,1,0:T(8,128)(2,1)S(1)}, bf16[16,16,512]{2,1,0:T(8,128)(2,1)}, u32[]{:S(2)}) copy-start(bf16[16,16,512]{2,1,0:T(8,128)(2,1)} %concatenate.33) | copy-start | bytes 786436
  61.6 1.2 copy-start.4
  62.5 4.8 %copy-start.2 = (f32[4,128,128]{1,2,0:T(8,128)S(1)}, f32[4,128,128]{1,2,0:T(8,128)}, u32[]{:S(2)}) copy-start(f32[4,128,128]{1,2,0:T(8,128)} %get-tuple-element.85) | copy-start | bytes 786436
  63.7 169.1 %all-to-all-start.1 = ((bf16[16,16,1024]{2,1,0:T(8,128)(2,1)}), bf16[16,16,1024]{2,1,0:T(8,128)(2,1)S(1)}, u32[]{:S(2)}, u32[]{:S(2)}) async-start(bf16[16,16,1024]{2,1,0:T(8,128)(2,1)} %pad_maximum_fusion), calls=%async_computation.1 | async-start | bytes 1048576 | tf_op jit(solution)/shard_map/all_to_all | solution.py:43
  68.7 2.5 %copy-start.12 = (f32[4,1,128,1]{2,1,3,0:T(1,128)S(1)}, f32[4,1,128,1]{2,1,3,0:T(1,128)}, u32[]{:S(2)}) copy-start(f32[4,1,128,1]{2,1,3,0:T(1,128)} %fusion.72) | copy-start | bytes 6148
where the time goes:
time: 234 us; the launch traced here: 233 us
  blocking collectives  161 us (69%)
  matrix products  22.1 us (9%)
  other arithmetic  15.1 us (6%)
  local copies, waits for them, and re-layouts  13.6 us (6%)
  waiting for transfers between devices  9.94 us (4%)
  starting transfers between devices  9.71 us (4%)
    psum x5, blocking collectives, by_axis(): return functools.reduce(lax.psum, axes, shard)  161 us
    all_to_all x1, waiting for transfers between devices, copy_for_each(): return lax.all_to_all(copies, axis, split_axis=0, concat_axis=0, tiled=True)  9.94 us
    all_to_all x1, starting transfers between devices, copy_for_each(): return lax.all_to_all(copies, axis, split_axis=0, concat_axis=0, tiled=True)  6.14 us
  transfers between devices with their start and end apart: 2, of which 1 were waited for; matrix products, arithmetic and copies ran while one was open for 3% of the time, Pallas kernels for 0%

commit v1 on v0

v1 whole, which is shorter than its diff:
```python
import jax
import jax.numpy as jnp
from jax import lax
from jax.experimental import pallas as pl
from jax.experimental.pallas import tpu as pltpu
from jax.sharding import Mesh
from jax.sharding import PartitionSpec as P

QH = 20
KVH = 4
HD = 128
RESP = 128
PRE = 256
KEYS = PRE + RESP
GROUP = QH // KVH
WIDTH = KVH * HD
GW = GROUP * HD
PEERS = 16
ROWS = PRE // PEERS
CHUNK = 2 * KVH * ROWS
FACTOR = HD ** (-0.5)
SCALE = FACTOR * 1.4426950408889634
GRP = ("grp_0", "grp_1", "grp_2")
DP = ("dp_0", "dp_1")
PLANE = ("grp_0", "grp_1", "grp_2", "dp_1")
COLUMN = "dp_0"
NEG_BIG = -1e30
VMEM_LIMIT = 24 * 1024 * 1024
BF16 = jnp.bfloat16
F32 = jnp.float32


def dot(a, b, contract):
    return lax.dot_general(a, b, (contract, ((), ())), preferred_element_type=F32)


def in_three(x):
    high = x.astype(BF16).astype(F32)
    rest = x - high
    middle = rest.astype(BF16).astype(F32)
    return high, middle, rest - middle


def stacked(ref):
    return jnp.concatenate([ref[:, h * HD:(h + 1) * HD] for h in range(GROUP)], 0)


def row_sum(weights, rows):
    parts = jnp.concatenate([*in_three(weights), jnp.zeros((5, weights.shape[1]), F32)], 0)
    return jnp.sum(dot(parts.astype(BF16), rows, ((1,), (0,))), 0, keepdims=True)


def biased(values, bias_ref, index):
    return (values.astype(F32) + bias_ref[pl.ds(index, 1), :]).astype(BF16)


def raw_pair(both, q, g):
    zero = jnp.zeros((RESP, HD), BF16)
    pair = jnp.concatenate([jnp.concatenate([q, zero], 1), jnp.concatenate([zero, g], 1)], 0)
    return dot(both, pair, ((1,), (1,)))


def own_kernel(len_ref, query_ref, grad_ref, k_ref, v_ref, qb_ref, kb_ref,
               q_ref, g_ref, own_ref, e_ref, dp_ref, stat_ref):
    j = pl.program_id(0)
    live = lax.broadcasted_iota(jnp.int32, (RESP, HD), 0) < len_ref[0, 0]
    for h in range(GROUP):
        cols = slice(h * HD, (h + 1) * HD)
        q_ref[:, cols] = biased(query_ref[:, cols], qb_ref, j * GROUP + h)
        g_ref[:, cols] = jnp.where(live, grad_ref[:, cols].astype(F32), 0.0).astype(BF16)
    keys = biased(k_ref[...], kb_ref, j)
    vals = biased(v_ref[...], kb_ref, KVH + j)
    col = pl.multiple_of(j * HD, HD)
    own_ref[:, pl.ds(col, HD)] = keys
    own_ref[:, pl.ds(col + WIDTH, HD)] = vals
    both = jnp.concatenate([keys, vals], 1)
    allow = lax.broadcasted_iota(jnp.int32, (RESP, RESP), 0) <= lax.broadcasted_iota(jnp.int32, (RESP, RESP), 1)
    for h in range(GROUP):
        cols = slice(h * HD, (h + 1) * HD)
        raw = raw_pair(both, q_ref[:, cols], g_ref[:, cols])
        s = jnp.where(allow, raw[:, :RESP], NEG_BIG)
        dp = raw[:, RESP:]
        top = jnp.max(s, 0, keepdims=True)
        e = jnp.exp2((s - top) * SCALE)
        e_ref[:, cols] = e
        dp_ref[:, cols] = dp
        stat_ref[0, 0:1, cols] = top
        stat_ref[0, 1:2, cols] = jnp.sum(e, 0, keepdims=True)
        stat_ref[0, 2:3, cols] = jnp.sum(e * dp, 0, keepdims=True)
        stat_ref[0, 3:8, cols] = jnp.zeros((5, HD), F32)


STEP = 64


def fold(x, how):
    return how(x.reshape(-1, 8, HD), 0)


def score_kernel(q_ref, g_ref, pk_ref, pv_ref, kb_ref, own_ref, e_ref, dp_ref, stat_ref, bias_ref, raw_ref, ds_ref):
    j = pl.program_id(0)
    keys = biased(pk_ref[...], kb_ref, j)
    both = jnp.concatenate([keys, biased(pv_ref[...], kb_ref, KVH + j)], 1)
    for h in range(GROUP):
        cols = slice(h * HD, (h + 1) * HD)
        raw_ref[h] = raw_pair(both, q_ref[:, cols], g_ref[:, cols])
    shift_sums = []
    prob_sums = []
    for h in range(GROUP):
        cols = slice(h * HD, (h + 1) * HD)
        own_top = stat_ref[0, 0:1, cols]
        high = jnp.full((8, HD), NEG_BIG, F32)
        for at in range(0, PRE, STEP):
            high = jnp.maximum(high, fold(raw_ref[h, at:at + STEP, :RESP], jnp.max))
        top = jnp.maximum(own_top, jnp.max(high, 0, keepdims=True))
        total = jnp.zeros((8, HD), F32)
        meet = jnp.zeros((8, HD), F32)
        for at in range(0, PRE, STEP):
            e = jnp.exp2((raw_ref[h, at:at + STEP, :RESP] - top) * SCALE)
            raw_ref[h, at:at + STEP, :RESP] = e
            total = total + fold(e, jnp.sum)
            meet = meet + fold(e * raw_ref[h, at:at + STEP, RESP:], jnp.sum)
        fade = jnp.exp2((own_top - top) * SCALE)
        inverse = 1.0 / (stat_ref[0, 1:2, cols] * fade + jnp.sum(total, 0, keepdims=True))
        row = (stat_ref[0, 2:3, cols] * fade + jnp.sum(meet, 0, keepdims=True)) * inverse
        own_inverse = fade * inverse
        prob_sum = jnp.zeros((8, HD), F32)
        shift_sum = jnp.zeros((8, HD), F32)
        for at in range(0, KEYS, STEP):
            if at < PRE:
                p = raw_ref[h, at:at + STEP, :RESP] * inverse
                dp = raw_ref[h, at:at + STEP, RESP:]
            else:
                p = e_ref[at - PRE:at - PRE + STEP, cols] * own_inverse
                dp = dp_ref[at - PRE:at - PRE + STEP, cols]
            pb = p.astype(BF16)
            dsb = (p * (dp - row)).astype(BF16)
            ds_ref[at:at + STEP, cols] = dsb
            prob_sum = prob_sum + fold(pb.astype(F32), jnp.sum)
            shift_sum = shift_sum + fold(dsb.astype(F32), jnp.sum)
        prob_sums.append(jnp.sum(prob_sum, 0, keepdims=True))
        shift_sums.append(jnp.sum(shift_sum, 0, keepdims=True))

    def put(index, value):
        for copy in range(2):
            bias_ref[pl.ds(2 * (index // 2) + copy, 1), pl.ds(index % 2, 1), :] = value.reshape(1, 1, HD)

    dq = dot(ds_ref[...], jnp.concatenate([keys, own_ref[...]], 0), ((0,), (0,))) * FACTOR
    for h in range(GROUP):
        put(j * GROUP + h, jnp.sum(dq[h * RESP:(h + 1) * RESP], 0, keepdims=True))
    put(QH + j, row_sum(jnp.concatenate(shift_sums, 1), stacked(q_ref)) * FACTOR)
    put(QH + KVH + j, row_sum(jnp.concatenate(prob_sums, 1), stacked(g_ref)))
    put(QH + 2 * KVH + j, jnp.zeros((1, HD), F32))


def grad_kernel(len_ref, q_ref, g_ref, pk_ref, pv_ref, kb_ref, ok_ref, ov_ref,
                att_ref, dq_ref, own_ref, pre_ref, pt_ref, ds_ref):
    j = pl.program_id(0)
    keys = jnp.concatenate([biased(pk_ref[...], kb_ref, j), ok_ref[...]], 0)
    vals = jnp.concatenate([biased(pv_ref[...], kb_ref, KVH + j), ov_ref[...]], 0)
    both = jnp.concatenate([keys, vals], 1)
    allow = lax.broadcasted_iota(jnp.int32, (RESP, RESP), 0) <= lax.broadcasted_iota(jnp.int32, (RESP, RESP), 1)
    for h in range(GROUP):
        cols = slice(h * HD, (h + 1) * HD)
        raw = raw_pair(both, q_ref[:, cols], g_ref[:, cols])
        s = raw[:, :RESP]
        dp = raw[:, RESP:]
        s = jnp.concatenate([s[:PRE], jnp.where(allow, s[PRE:], NEG_BIG)], 0)
        e = jnp.exp2((s - jnp.max(s, 0, keepdims=True)) * SCALE)
        p = e * (1.0 / jnp.sum(e, 0, keepdims=True))
        row = jnp.sum(p * dp, 0, keepdims=True)
        pt_ref[:, cols] = p.astype(BF16)
        ds_ref[:, cols] = (p * (dp - row)).astype(BF16)
    pt = pt_ref[...]
    ds = ds_ref[...]
    dk = dot(ds, stacked(q_ref), ((1,), (0,))) * FACTOR
    dv = dot(pt, stacked(g_ref), ((1,), (0,)))
    col = pl.multiple_of(j * HD, HD)
    own_ref[:, pl.ds(col, HD)] = dk[PRE:].astype(BF16)
    own_ref[:, pl.ds(col + WIDTH, HD)] = dv[PRE:].astype(BF16)
    at = pl.multiple_of(j * ROWS, ROWS)
    pre_ref[:, pl.ds(at, ROWS), :] = dk[:PRE].astype(BF16).reshape(PEERS, ROWS, HD)
    pre_ref[:, pl.ds(at + KVH * ROWS, ROWS), :] = dv[:PRE].astype(BF16).reshape(PEERS, ROWS, HD)
    dq = dot(ds, keys, ((0,), (0,))) * FACTOR
    out = dot(pt, vals, ((0,), (0,)))
    live = lax.broadcasted_iota(jnp.int32, (RESP, HD), 0) < len_ref[0, 0]
    for h in range(GROUP):
        cols = slice(h * HD, (h + 1) * HD)
        rows = slice(h * RESP, (h + 1) * RESP)
        att_ref[:, cols] = jnp.where(live, out[rows], 0.0).astype(BF16)
        dq_ref[:, cols] = dq[rows].astype(BF16)


def enclose_kernel(buffer_ref, parts_ref, out_ref):
    del buffer_ref
    total = jnp.sum(parts_ref[...], 0)
    rows = jnp.concatenate([*in_three(total), jnp.zeros((2, HD), F32)], 0).astype(BF16)
    out_ref[...] = jnp.broadcast_to(rows[None], (PEERS, 8, HD))


def finish_kernel(arrived_ref, pre_ref, q_ref, kv_ref):
    for m in range(2 * KVH):
        piece = arrived_ref[:, m * ROWS:(m + 1) * ROWS, :].astype(F32)
        pre_ref[:, m * HD:(m + 1) * HD] = jnp.sum(piece, 0).astype(BF16)
    for i in range((QH + 2 * KVH) // 2):
        tail = arrived_ref[i, CHUNK:, :].astype(F32)
        pair = tail[0:2] + tail[2:4] + tail[4:6]
        if 2 * i < QH:
            q_ref[2 * i:2 * i + 2, :] = pair
        else:
            kv_ref[2 * i - QH:2 * i - QH + 2, :] = pair


def first(j):
    return 0, j


def second(j):
    return 0, KVH + j


def whole(j):
    return 0, 0


def params():
    return pltpu.CompilerParams(dimension_semantics=("arbitrary",), vmem_limit_bytes=VMEM_LIMIT)


def cost(matmuls):
    return pl.CostEstimate(
        flops=matmuls * 2 * QH * RESP * KEYS * HD, bytes_accessed=4_000_000, transcendentals=QH * RESP * KEYS
    )


def own(length, query, out_grad, resp_kv, query_bias, kv_bias):
    wide = pl.BlockSpec((RESP, GW), first)
    return pl.pallas_call(
        own_kernel,
        grid=(KVH,),
        in_specs=[
            pl.BlockSpec(memory_space=pltpu.SMEM),
            wide,
            wide,
            pl.BlockSpec((RESP, HD), first),
            pl.BlockSpec((RESP, HD), second),
            pl.BlockSpec((QH, HD), whole),
            pl.BlockSpec((2 * KVH, HD), whole),
        ],
        out_specs=[
            wide,
            wide,
            pl.BlockSpec((RESP, 2 * WIDTH), lambda j: (0, 0)),
            wide,
            wide,
            pl.BlockSpec((1, 8, GW), lambda j: (j, 0, 0)),
        ],
        out_shape=[
            jax.ShapeDtypeStruct((RESP, QH * HD), BF16),
            jax.ShapeDtypeStruct((RESP, QH * HD), BF16),
            jax.ShapeDtypeStruct((RESP, 2 * WIDTH), BF16),
            pltpu.HBM((RESP, QH * HD), F32),
            pltpu.HBM((RESP, QH * HD), F32),
            jax.ShapeDtypeStruct((KVH, 8, GW), F32),
        ],
        compiler_params=params(),
        cost_estimate=cost(1),
        name="own",
    )(length, query, out_grad, resp_kv, resp_kv, query_bias, kv_bias)


def score(q, g, prefix, kv_bias, own_kv, e, dp, stat):
    wide = pl.BlockSpec((RESP, GW), first)
    return pl.pallas_call(
        score_kernel,
        grid=(KVH,),
        in_specs=[
            wide,
            wide,
            pl.BlockSpec((PRE, HD), first),
            pl.BlockSpec((PRE, HD), second),
            pl.BlockSpec((2 * KVH, HD), whole),
            pl.BlockSpec((RESP, HD), first),
            wide,
            wide,
            pl.BlockSpec((1, 8, GW), lambda j: (j, 0, 0)),
        ],
        out_specs=pl.BlockSpec((32, 2, HD), lambda j: (0, 0, 0)),
        out_shape=jax.ShapeDtypeStruct((32, 2, HD), F32),
        scratch_shapes=[pltpu.VMEM((GROUP, PRE, 2 * RESP), F32), pltpu.VMEM((KEYS, GW), BF16)],
        compiler_params=params(),
        cost_estimate=cost(3),
        name="score",
    )(q, g, prefix, prefix, kv_bias, own_kv, e, dp, stat)


def grads(length, q, g, prefix, kv_bias, own_kv):
    wide = pl.BlockSpec((RESP, GW), first)
    return pl.pallas_call(
        grad_kernel,
        grid=(KVH,),
        in_specs=[
            pl.BlockSpec(memory_space=pltpu.SMEM),
            wide,
            wide,
            pl.BlockSpec((PRE, HD), first),
            pl.BlockSpec((PRE, HD), second),
            pl.BlockSpec((2 * KVH, HD), whole),
            pl.BlockSpec((RESP, HD), first),
            pl.BlockSpec((RESP, HD), second),
        ],
        out_specs=[
            wide,
            wide,
            pl.BlockSpec((RESP, 2 * WIDTH), whole),
            pl.BlockSpec((PEERS, CHUNK + 8, HD), lambda j: (0, 0, 0)),
        ],
        out_shape=[
            jax.ShapeDtypeStruct((RESP, QH * HD), BF16),
            jax.ShapeDtypeStruct((RESP, QH * HD), BF16),
            jax.ShapeDtypeStruct((RESP, 2 * WIDTH), BF16),
            jax.ShapeDtypeStruct((PEERS, CHUNK + 8, HD), BF16),
        ],
        scratch_shapes=[pltpu.VMEM((KEYS, GW), BF16), pltpu.VMEM((KEYS, GW), BF16)],
        compiler_params=params(),
        cost_estimate=cost(6),
        name="grads",
    )(length, q, g, prefix, prefix, kv_bias, own_kv, own_kv)


def enclose(pre, parts):
    return pl.pallas_call(
        enclose_kernel,
        grid=(1,),
        in_specs=[pl.BlockSpec(memory_space=pl.ANY), pl.BlockSpec((32, 2, HD), lambda i: (0, 0, 0))],
        out_specs=pl.BlockSpec((PEERS, 8, HD), lambda i: (0, CHUNK // 8, 0)),
        out_shape=jax.ShapeDtypeStruct(pre.shape, BF16),
        input_output_aliases={0: 0},
        compiler_params=params(),
        name="enclose",
    )(pre, parts)


def finish(arrived):
    return pl.pallas_call(
        finish_kernel,
        out_shape=[
            jax.ShapeDtypeStruct((ROWS, 2 * WIDTH), BF16),
            jax.ShapeDtypeStruct((QH, HD), F32),
            jax.ShapeDtypeStruct((2 * KVH, HD), F32),
        ],
        compiler_params=pltpu.CompilerParams(vmem_limit_bytes=VMEM_LIMIT),
        name="finish",
    )(arrived)


def in_hbm(x):
    return pltpu.with_memory_space_constraint(x, pltpu.HBM)


def exchange(pieces, axes):
    return lax.all_to_all(pieces, axes, 0, 0, tiled=True)


def local(query, resp_kv, prefix_kv, query_bias, kv_bias, out_grad, lengths):
    query_bias = query_bias.reshape(QH, HD)
    kv_bias = kv_bias.reshape(2 * KVH, HD)
    prefix = exchange(jnp.broadcast_to(prefix_kv[0], (PEERS, ROWS, 2 * WIDTH)), GRP).reshape(PRE, 2 * WIDTH)
    q, g, own_kv, e, dp, stat = own(lengths, in_hbm(query[0]), in_hbm(out_grad[0]), in_hbm(resp_kv[0]), query_bias, kv_bias)
    bias = score(q, g, prefix, kv_bias, own_kv, in_hbm(e), in_hbm(dp), stat)
    part = jnp.sum(exchange(bias, PLANE), 0)
    part, lengths = lax.optimization_barrier((part, lengths))
    att, dq, own_grad, pre = grads(lengths, q, g, prefix, kv_bias, own_kv)
    part = exchange(jnp.broadcast_to(part, (32, 2, HD)), COLUMN)
    pre_grad, qsum, kvsum = finish(exchange(enclose(pre, part), GRP))
    return (
        att[None],
        dq[None],
        own_grad[None],
        pre_grad[None],
        qsum.reshape(QH * HD),
        kvsum.reshape(2 * WIDTH),
    )


def solution(mesh):
    finer = Mesh(mesh.devices.reshape(2, 4, 2, 32, 2), ("grp_0", "grp_1", "grp_2", "dp_0", "dp_1"))
    rows = P(DP, GRP, None)
    return jax.shard_map(
        local,
        mesh=finer,
        in_specs=(rows, rows, rows, P(), P(), rows, P(DP, GRP)),
        out_specs=(rows, rows, rows, rows, P(), P()),
        check_vma=False,
    )
```

time: 234 us -> 108 us (0.46)
  the two profiles are of different devices: /device:TPU:8 before, /device:TPU:1 now
where the time goes in v1:
time: 108 us
  starting transfers between devices  36.8 us (34%)
  blocking collectives  28.7 us (27%)
  waiting for transfers between devices  20.3 us (19%)
  Pallas kernels  18.5 us (17%)
  local copies, waits for them, and re-layouts  2.26 us (2%)
  between operations  1.34 us (1%)
    all_to_all x2, starting transfers between devices, exchange(): return lax.all_to_all(pieces, axes, 0, 0, tiled=True)  36.8 us
    all_to_all x2, blocking collectives, exchange(): return lax.all_to_all(pieces, axes, 0, 0, tiled=True)  28.7 us
    all_to_all x2, waiting for transfers between devices, exchange(): return lax.all_to_all(pieces, axes, 0, 0, tiled=True)  20.3 us
    pallas_call x1, Pallas kernels, grads(): pl.pallas_call(grad_kernel, grid=(KVH,), in_specs=[pl.BlockSpec(memory_sp...  7.35 us
    pallas_call x1, Pallas kernels, score(): pl.pallas_call(score_kernel, grid=(KVH,), in_specs=[wide, wide, pl.BlockS...  5.6 us
    pallas_call x1, Pallas kernels, own(): pl.pallas_call(own_kernel, grid=(KVH,), in_specs=[pl.BlockSpec(memory_spa...  4.76 us
  transfers between devices with their start and end apart: 2, of which 2 were waited for; matrix products, arithmetic and copies ran while one was open for 0% of the time, Pallas kernels for 11%

profile of v1, /device:TPU:1, one launch (start us, length us, event | category | flops | bytes accessed | tf_op | source)
XLA Modules:
  0.0 107.9 jit_solution(7740095024861188331)
XLA Ops:
  0.6 0.0 copy-start
  0.6 0.0 copy-start.1
  0.7 1.6 %broadcast_in_dim.18 = bf16[16,16,1024]{2,1,0:T(8,128)(2,1)} broadcast(bf16[16,1024]{1,0:T(8,128)(2,1)} %bitcast.21), dimensions={1,2} | broadcast | bytes 557056 | tf_op jit(solution)/shard_map/broadcast_in_dim | solution.py:368
  2.3 17.5 %all-to-all-start = ((bf16[16,16,1024]{2,1,0:T(8,128)(2,1)}), bf16[16,16,1024]{2,1,0:T(8,128)(2,1)S(1)}, u32[]{:S(2)}, u32[]{:S(2)}) async-start(bf16[16,16,1024]{2,1,0:T(8,128)(2,1)} %broadcast_in_dim.18), calls=%async_computation | async-start | bytes 1048576 | tf_op jit(solution)/shard_map/all_to_all | solution.py:362
  20.4 0.0 copy-done
  20.4 0.0 copy-done.1
  20.4 4.8 %own.1 = (bf16[128,2560]{1,0:T(8,128)(2,1)S(1)}, bf16[128,2560]{1,0:T(8,128)(2,1)S(1)}, bf16[128,1024]{1,0:T(8,128)(2,1)S(1)}, f32[128,2560]{1,0:T(8,128)}, f32[...) custom-call(s32[1,1]{1,0:T(1,128)S(6)} %copy.15.len_ref, bf16[128,2560]{1,0:T(8,128)(2,1)} %bitcast.22, ...), custom_call_target="tpu_custom_call" | custom-call | flops 251658240 | bytes 4000000 | tf_op jit(solution)/shard_map/own/pallas_call | solution.py:238
  25.2 5.7 %all-to-all-done = bf16[16,16,1024]{2,1,0:T(8,128)(2,1)S(1)} async-done(((bf16[16,16,1024]{2,1,0:T(8,128)(2,1)}), bf16[16,16,1024]{2,1,0:T(8,128)(2,1)S(1)}, u32[]{:S(2)}, u32[]{:S(2)}) %all-to-all-start) | async-done | bytes 524320 | tf_op jit(solution)/shard_map/all_to_all | solution.py:362
  30.9 5.6 %score.1 = f32[32,2,128]{2,1,0:T(2,128)S(1)} custom-call(bf16[128,2560]{1,0:T(8,128)(2,1)S(1)} %get-tuple-element.21.q_ref, bf16[128,2560]{1,0:T(8,128)(2,1)S(1)} %get-tuple-element.22.g_ref, bf16[256,1024]{1,0:T(8,128)(2,1)S(1)} %bitcast.13, bf16[256,1024]{1,0:T(8,128)(2,1)S(1)} %bitcast.14, f32[8,128]{1,0:T(8,128)S(1)} %bitcast.18, ...), custom_call_target="tpu_custom_call" | custom-call | flops 754974720 | bytes 4000000 | tf_op jit(solution)/shard_map/score/pallas_call | solution.py:274
  36.5 11.2 %all_to_all.20 = f32[32,2,128]{2,1,0:T(2,128)S(1)} all-to-all(f32[32,2,128]{2,1,0:T(2,128)S(1)} %score.1), channel_id=1, replica_groups=mesh['grp_0'=2,'grp_1'=4,'grp_2'=2,'dp_0'=32,'dp_1'=2] {'grp_0','grp_1',..., dimensions={0} | all-to-all | bytes 65536 | tf_op jit(solution)/shard_map/all_to_all | solution.py:362
  47.7 0.6 broadcast_in_dim.22
  48.3 19.3 %all-to-all-start.2 = ((f32[32,2,128]{2,1,0:T(2,128)}), f32[32,2,128]{2,1,0:T(2,128)S(1)}, u32[]{:S(2)}, u32[]{:S(2)}) async-start(f32[32,2,128]{2,1,0:T(2,128)} %broadcast_in_dim.22), calls=%async_computation.2 | async-start | bytes 65536 | tf_op jit(solution)/shard_map/all_to_all | solution.py:362
  67.7 7.4 %grads.1 = (bf16[128,2560]{1,0:T(8,128)(2,1)}, bf16[128,2560]{1,0:T(8,128)(2,1)}, bf16[128,1024]{1,0:T(8,128)(2,1)}, bf16[16,136,128]{2,1,0:T(8,128)(2,1)S(1)}) custom-call(s32[1,1]{1,0:T(1,128)S(6)} %copy.15.len_ref, bf16[128,2560]{1,0:T(8,128)(2,1)S(1)} %get-tuple-element.21.q_ref, bf16[128,2560]{1,0:T(8,128)(2,1)S(1)} %get-tuple-element.22.g_ref, ...), custom_call_target="tpu_custom_call" | custom-call | flops 1509949440 | bytes 4000000 | tf_op jit(solution)/shard_map/grads/pallas_call | solution.py:299
  75.0 14.7 %all-to-all-done.2.parts_ref = f32[32,2,128]{2,1,0:T(2,128)S(1)} async-done(((f32[32,2,128]{2,1,0:T(2,128)}), f32[32,2,128]{2,1,0:T(2,128)S(1)}, u32[]{:S(2)}, u32[]{:S(2)}) %all-to-all-start.2) | async-done | bytes 32800 | tf_op jit(solution)/shard_map/all_to_all | solution.py:362
  89.7 0.1 enclose.1
  89.7 17.5 %all_to_all.21.arrived_ref = bf16[16,136,128]{2,1,0:T(8,128)(2,1)S(1)} all-to-all(bf16[16,136,128]{2,1,0:T(8,128)(2,1)S(1)} %enclose.1), channel_id=1, replica_groups=mesh['grp_0'=2,'grp_1'=4,'grp_2'=2,'dp_0'=32,'dp_1'=2] {'grp_0','grp_1',..., dimensions={0} | all-to-all | bytes 1114112 | tf_op jit(solution)/shard_map/all_to_all | solution.py:362
  107.2 0.7 finish.1
  (1 shorter events, 0.0 us)
Async XLA Ops:
  0.6 19.8 %copy-start = (f32[1024]{0:T(1024)S(1)}, f32[1024]{0:T(1024)}, u32[]{:S(2)}) copy-start(f32[1024]{0:T(1024)} %param.11) | copy-start | bytes 12292
  0.6 19.8 %copy-start.1 = (f32[2560]{0:T(1024)S(1)}, f32[2560]{0:T(1024)}, u32[]{:S(2)}) copy-start(f32[2560]{0:T(1024)} %param.10) | copy-start | bytes 30724
  2.3 28.6 %all-to-all-start = ((bf16[16,16,1024]{2,1,0:T(8,128)(2,1)}), bf16[16,16,1024]{2,1,0:T(8,128)(2,1)S(1)}, u32[]{:S(2)}, u32[]{:S(2)}) async-start(bf16[16,16,1024]{2,1,0:T(8,128)(2,1)} %broadcast_in_dim.18), calls=%async_computation | async-start | bytes 1048576 | tf_op jit(solution)/shard_map/all_to_all | solution.py:362
  48.3 41.4 %all-to-all-start.2 = ((f32[32,2,128]{2,1,0:T(2,128)}), f32[32,2,128]{2,1,0:T(2,128)S(1)}, u32[]{:S(2)}, u32[]{:S(2)}) async-start(f32[32,2,128]{2,1,0:T(2,128)} %broadcast_in_dim.22), calls=%async_computation.2 | async-start | bytes 65536 | tf_op jit(solution)/shard_map/all_to_all | solution.py:362

commit v2 on v1

--- a/solution.py
+++ b/solution.py
@@ -371,7 +371,10 @@
     part = jnp.sum(exchange(bias, PLANE), 0)
     part, lengths = lax.optimization_barrier((part, lengths))
     att, dq, own_grad, pre = grads(lengths, q, g, prefix, kv_bias, own_kv)
-    part = exchange(jnp.broadcast_to(part, (32, 2, HD)), COLUMN)
+    order = [(i + 20) % 32 for i in range(32)]
+    part = lax.all_to_all(
+        jnp.broadcast_to(part, (32, 2, HD)), COLUMN, 0, 0, axis_index_groups=[order], tiled=True
+    )
     pre_grad, qsum, kvsum = finish(exchange(enclose(pre, part), GRP))
     return (
         att[None],

time: 108 us -> 96 us (0.89)
  waiting for transfers between devices: 20.3 us -> 6.04 us
  starting transfers between devices: 36.8 us -> 38.9 us
    all_to_all x0 -> x1, starting transfers between devices: none -> 21.4 us  [local(): lax.all_to_all(jnp.broadcast_to(part, (32, 2, HD)), COLUMN, 0, 0, axis_in...]
    all_to_all x2 -> x1, starting transfers between devices: 36.8 us -> 17.5 us  [exchange(): return lax.all_to_all(pieces, axes, 0, 0, tiled=True)]
    all_to_all x2 -> x1, waiting for transfers between devices: 20.3 us -> 5.67 us  [exchange(): return lax.all_to_all(pieces, axes, 0, 0, tiled=True)]
  transfers between devices with their start and end apart: 2 -> 2, of which waited for: 2 -> 2; matrix products, arithmetic and copies ran while one was open for 0% -> 0% of each run, Pallas kernels for 11% -> 13%
where the time goes in v2:
time: 96 us; the launch traced here: 95.4 us
  starting transfers between devices  38.9 us (41%)
  blocking collectives  28.4 us (30%)
  Pallas kernels  18.5 us (19%)
  waiting for transfers between devices  6.04 us (6%)
  local copies, waits for them, and re-layouts  2.26 us (2%)
  between operations  1.34 us (1%)
    all_to_all x2, blocking collectives, exchange(): return lax.all_to_all(pieces, axes, 0, 0, tiled=True)  28.4 us
    all_to_all x1, starting transfers between devices, local(): lax.all_to_all(jnp.broadcast_to(part, (32, 2, HD)), COLUMN, 0, 0, axis_in...  21.4 us
    all_to_all x1, starting transfers between devices, exchange(): return lax.all_to_all(pieces, axes, 0, 0, tiled=True)  17.5 us
    pallas_call x1, Pallas kernels, grads(): pl.pallas_call(grad_kernel, grid=(KVH,), in_specs=[pl.BlockSpec(memory_sp...  7.36 us
    all_to_all x1, waiting for transfers between devices, exchange(): return lax.all_to_all(pieces, axes, 0, 0, tiled=True)  5.67 us
    pallas_call x1, Pallas kernels, score(): pl.pallas_call(score_kernel, grid=(KVH,), in_specs=[wide, wide, pl.BlockS...  5.6 us
    pallas_call x1, Pallas kernels, own(): pl.pallas_call(own_kernel, grid=(KVH,), in_specs=[pl.BlockSpec(memory_spa...  4.76 us
  transfers between devices with their start and end apart: 2, of which 2 were waited for; matrix products, arithmetic and copies ran while one was open for 0% of the time, Pallas kernels for 13%

profile of v2, /device:TPU:1, one launch (start us, length us, event | category | flops | bytes accessed | tf_op | source)
XLA Modules:
  0.0 95.4 jit_solution(3878700873509519265)
XLA Ops:
  0.6 0.0 copy-start
  0.6 0.0 copy-start.1
  0.7 1.6 %broadcast_in_dim.18 = bf16[16,16,1024]{2,1,0:T(8,128)(2,1)} broadcast(bf16[16,1024]{1,0:T(8,128)(2,1)} %bitcast.21), dimensions={1,2} | broadcast | bytes 557056 | tf_op jit(solution)/shard_map/broadcast_in_dim | solution.py:368
  2.3 17.5 %all-to-all-start = ((bf16[16,16,1024]{2,1,0:T(8,128)(2,1)}), bf16[16,16,1024]{2,1,0:T(8,128)(2,1)S(1)}, u32[]{:S(2)}, u32[]{:S(2)}) async-start(bf16[16,16,1024]{2,1,0:T(8,128)(2,1)} %broadcast_in_dim.18), calls=%async_computation | async-start | bytes 1048576 | tf_op jit(solution)/shard_map/all_to_all | solution.py:362
  20.4 0.0 copy-done
  20.4 0.0 copy-done.1
  20.4 4.8 %own.1 = (bf16[128,2560]{1,0:T(8,128)(2,1)S(1)}, bf16[128,2560]{1,0:T(8,128)(2,1)S(1)}, bf16[128,1024]{1,0:T(8,128)(2,1)S(1)}, f32[128,2560]{1,0:T(8,128)}, f32[...) custom-call(s32[1,1]{1,0:T(1,128)S(6)} %copy.15.len_ref, bf16[128,2560]{1,0:T(8,128)(2,1)} %bitcast.22, ...), custom_call_target="tpu_custom_call" | custom-call | flops 251658240 | bytes 4000000 | tf_op jit(solution)/shard_map/own/pallas_call | solution.py:238
  25.2 5.7 %all-to-all-done = bf16[16,16,1024]{2,1,0:T(8,128)(2,1)S(1)} async-done(((bf16[16,16,1024]{2,1,0:T(8,128)(2,1)}), bf16[16,16,1024]{2,1,0:T(8,128)(2,1)S(1)}, u32[]{:S(2)}, u32[]{:S(2)}) %all-to-all-start) | async-done | bytes 524320 | tf_op jit(solution)/shard_map/all_to_all | solution.py:362
  30.9 5.6 %score.1 = f32[32,2,128]{2,1,0:T(2,128)S(1)} custom-call(bf16[128,2560]{1,0:T(8,128)(2,1)S(1)} %get-tuple-element.21.q_ref, bf16[128,2560]{1,0:T(8,128)(2,1)S(1)} %get-tuple-element.22.g_ref, bf16[256,1024]{1,0:T(8,128)(2,1)S(1)} %bitcast.13, bf16[256,1024]{1,0:T(8,128)(2,1)S(1)} %bitcast.14, f32[8,128]{1,0:T(8,128)S(1)} %bitcast.18, ...), custom_call_target="tpu_custom_call" | custom-call | flops 754974720 | bytes 4000000 | tf_op jit(solution)/shard_map/score/pallas_call | solution.py:274
  36.5 11.2 %all_to_all.20 = f32[32,2,128]{2,1,0:T(2,128)S(1)} all-to-all(f32[32,2,128]{2,1,0:T(2,128)S(1)} %score.1), channel_id=1, replica_groups=mesh['grp_0'=2,'grp_1'=4,'grp_2'=2,'dp_0'=32,'dp_1'=2] {'grp_0','grp_1',..., dimensions={0} | all-to-all | bytes 65536 | tf_op jit(solution)/shard_map/all_to_all | solution.py:362
  47.7 0.6 broadcast_in_dim.22
  48.3 21.4 %all-to-all-start.2 = ((f32[32,2,128]{2,1,0:T(2,128)}), f32[32,2,128]{2,1,0:T(2,128)S(1)}, u32[]{:S(2)}, u32[]{:S(2)}) async-start(f32[32,2,128]{2,1,0:T(2,128)} %broadcast_in_dim.22), calls=%async_computation.2 | async-start | bytes 65536 | tf_op jit(solution)/shard_map/all_to_all | solution.py:375
  69.7 7.4 %grads.1 = (bf16[128,2560]{1,0:T(8,128)(2,1)}, bf16[128,2560]{1,0:T(8,128)(2,1)}, bf16[128,1024]{1,0:T(8,128)(2,1)}, bf16[16,136,128]{2,1,0:T(8,128)(2,1)S(1)}) custom-call(s32[1,1]{1,0:T(1,128)S(6)} %copy.15.len_ref, bf16[128,2560]{1,0:T(8,128)(2,1)S(1)} %get-tuple-element.21.q_ref, bf16[128,2560]{1,0:T(8,128)(2,1)S(1)} %get-tuple-element.22.g_ref, ...), custom_call_target="tpu_custom_call" | custom-call | flops 1509949440 | bytes 4000000 | tf_op jit(solution)/shard_map/grads/pallas_call | solution.py:299
  77.1 0.4 all-to-all-done.2.parts_ref
  77.5 0.1 enclose.1
  77.5 17.2 %all_to_all.21.arrived_ref = bf16[16,136,128]{2,1,0:T(8,128)(2,1)S(1)} all-to-all(bf16[16,136,128]{2,1,0:T(8,128)(2,1)S(1)} %enclose.1), channel_id=1, replica_groups=mesh['grp_0'=2,'grp_1'=4,'grp_2'=2,'dp_0'=32,'dp_1'=2] {'grp_0','grp_1',..., dimensions={0} | all-to-all | bytes 1114112 | tf_op jit(solution)/shard_map/all_to_all | solution.py:362
  94.7 0.7 finish.1
  (1 shorter events, 0.0 us)
Async XLA Ops:
  0.6 19.8 %copy-start = (f32[1024]{0:T(1024)S(1)}, f32[1024]{0:T(1024)}, u32[]{:S(2)}) copy-start(f32[1024]{0:T(1024)} %param.11) | copy-start | bytes 12292
  0.6 19.8 %copy-start.1 = (f32[2560]{0:T(1024)S(1)}, f32[2560]{0:T(1024)}, u32[]{:S(2)}) copy-start(f32[2560]{0:T(1024)} %param.10) | copy-start | bytes 30724
  2.3 28.6 %all-to-all-start = ((bf16[16,16,1024]{2,1,0:T(8,128)(2,1)}), bf16[16,16,1024]{2,1,0:T(8,128)(2,1)S(1)}, u32[]{:S(2)}, u32[]{:S(2)}) async-start(bf16[16,16,1024]{2,1,0:T(8,128)(2,1)} %broadcast_in_dim.18), calls=%async_computation | async-start | bytes 1048576 | tf_op jit(solution)/shard_map/all_to_all | solution.py:362
  48.3 29.2 %all-to-all-start.2 = ((f32[32,2,128]{2,1,0:T(2,128)}), f32[32,2,128]{2,1,0:T(2,128)S(1)}, u32[]{:S(2)}, u32[]{:S(2)}) async-start(f32[32,2,128]{2,1,0:T(2,128)} %broadcast_in_dim.22), calls=%async_computation.2 | async-start | bytes 65536 | tf_op jit(solution)/shard_map/all_to_all | solution.py:375

commit v3 on v2

--- a/solution.py
+++ b/solution.py
@@ -1,3 +1,5 @@
+import functools
+
 import jax
 import jax.numpy as jnp
 from jax import lax
@@ -25,6 +27,7 @@
 PLANE = ("grp_0", "grp_1", "grp_2", "dp_1")
 COLUMN = "dp_0"
 NEG_BIG = -1e30
+FIRST = 2
 VMEM_LIMIT = 24 * 1024 * 1024
 BF16 = jnp.bfloat16
 F32 = jnp.float32
@@ -104,8 +107,11 @@
     for h in range(GROUP):
         cols = slice(h * HD, (h + 1) * HD)
         raw_ref[h] = raw_pair(both, q_ref[:, cols], g_ref[:, cols])
-    shift_sums = []
-    prob_sums = []
+    all_keys = jnp.concatenate([keys, own_ref[...]], 0)
+    ones = jnp.ones((8, RESP), BF16)
+    key_weights = []
+    key_sum = jnp.zeros((1, HD), F32)
+    value_sum = jnp.zeros((1, HD), F32)
     for h in range(GROUP):
         cols = slice(h * HD, (h + 1) * HD)
         own_top = stat_ref[0, 0:1, cols]
@@ -138,24 +144,34 @@
             ds_ref[at:at + STEP, cols] = dsb
             prob_sum = prob_sum + fold(pb.astype(F32), jnp.sum)
             shift_sum = shift_sum + fold(dsb.astype(F32), jnp.sum)
-        prob_sums.append(jnp.sum(prob_sum, 0, keepdims=True))
-        shift_sums.append(jnp.sum(shift_sum, 0, keepdims=True))
+        key_weights.append(dot(ones, ds_ref[:, cols], ((1,), (1,)))[0:1])
+        key_sum = key_sum + row_sum(jnp.sum(shift_sum, 0, keepdims=True), q_ref[:, cols])
+        value_sum = value_sum + row_sum(jnp.sum(prob_sum, 0, keepdims=True), g_ref[:, cols])
 
     def put(index, value):
         for copy in range(2):
             bias_ref[pl.ds(2 * (index // 2) + copy, 1), pl.ds(index % 2, 1), :] = value.reshape(1, 1, HD)
 
-    dq = dot(ds_ref[...], jnp.concatenate([keys, own_ref[...]], 0), ((0,), (0,))) * FACTOR
-    for h in range(GROUP):
-        put(j * GROUP + h, jnp.sum(dq[h * RESP:(h + 1) * RESP], 0, keepdims=True))
-    put(QH + j, row_sum(jnp.concatenate(shift_sums, 1), stacked(q_ref)) * FACTOR)
-    put(QH + KVH + j, row_sum(jnp.concatenate(prob_sums, 1), stacked(g_ref)))
+    parts = [*in_three(jnp.concatenate(key_weights, 0)), jnp.zeros((1, KEYS), F32)]
+    query_sum = dot(jnp.concatenate(parts, 0).astype(BF16), all_keys, ((1,), (0,)))
+    for h in range(GROUP):
+        mine = query_sum[h:h + 1] + query_sum[GROUP + h:GROUP + h + 1] + query_sum[2 * GROUP + h:2 * GROUP + h + 1]
+        put(j * GROUP + h, mine * FACTOR)
+    put(QH + j, key_sum * FACTOR)
+    put(QH + KVH + j, value_sum)
     put(QH + 2 * KVH + j, jnp.zeros((1, HD), F32))
 
 
-def grad_kernel(len_ref, q_ref, g_ref, pk_ref, pv_ref, kb_ref, ok_ref, ov_ref,
-                att_ref, dq_ref, own_ref, pre_ref, pt_ref, ds_ref):
-    j = pl.program_id(0)
+def grad_kernel(base, len_ref, q_ref, g_ref, pk_ref, pv_ref, kb_ref, ok_ref, ov_ref, *rest):
+    *before, att_ref, dq_ref, own_ref, pre_ref, pt_ref, ds_ref = rest
+    j = base + pl.program_id(0)
+    if before:
+
+        @pl.when(j == base)
+        def _():
+            own_ref[...] = before[2][...]
+            pre_ref[...] = before[3][...]
+
     keys = jnp.concatenate([biased(pk_ref[...], kb_ref, j), ok_ref[...]], 0)
     vals = jnp.concatenate([biased(pv_ref[...], kb_ref, KVH + j), ov_ref[...]], 0)
     both = jnp.concatenate([keys, vals], 1)
@@ -229,7 +245,7 @@
 
 def cost(matmuls):
     return pl.CostEstimate(
-        flops=matmuls * 2 * QH * RESP * KEYS * HD, bytes_accessed=4_000_000, transcendentals=QH * RESP * KEYS
+        flops=int(matmuls * 2 * QH * RESP * KEYS * HD), bytes_accessed=4_000_000, transcendentals=QH * RESP * KEYS
     )
 
 
@@ -294,27 +310,34 @@
     )(q, g, prefix, prefix, kv_bias, own_kv, e, dp, stat)
 
 
-def grads(length, q, g, prefix, kv_bias, own_kv):
-    wide = pl.BlockSpec((RESP, GW), first)
+def grads(base, count, length, q, g, prefix, kv_bias, own_kv, *results):
+    def low(j):
+        return 0, base + j
+
+    def high(j):
+        return 0, KVH + base + j
+
+    wide = pl.BlockSpec((RESP, GW), low)
+    rest = [
+        pl.BlockSpec((RESP, 2 * WIDTH), whole),
+        pl.BlockSpec((PEERS, CHUNK + 8, HD), lambda j: (0, 0, 0)),
+    ]
+    anywhere = pl.BlockSpec(memory_space=pl.ANY)
     return pl.pallas_call(
-        grad_kernel,
-        grid=(KVH,),
+        functools.partial(grad_kernel, base),
+        grid=(count,),
         in_specs=[
             pl.BlockSpec(memory_space=pltpu.SMEM),
             wide,
             wide,
-            pl.BlockSpec((PRE, HD), first),
-            pl.BlockSpec((PRE, HD), second),
+            pl.BlockSpec((PRE, HD), low),
+            pl.BlockSpec((PRE, HD), high),
             pl.BlockSpec((2 * KVH, HD), whole),
-            pl.BlockSpec((RESP, HD), first),
-            pl.BlockSpec((RESP, HD), second),
-        ],
-        out_specs=[
-            wide,
-            wide,
-            pl.BlockSpec((RESP, 2 * WIDTH), whole),
-            pl.BlockSpec((PEERS, CHUNK + 8, HD), lambda j: (0, 0, 0)),
-        ],
+            pl.BlockSpec((RESP, HD), low),
+            pl.BlockSpec((RESP, HD), high),
+            *([anywhere, anywhere, *rest] if results else []),
+        ],
+        out_specs=[wide, wide, *rest],
         out_shape=[
             jax.ShapeDtypeStruct((RESP, QH * HD), BF16),
             jax.ShapeDtypeStruct((RESP, QH * HD), BF16),
@@ -322,10 +345,11 @@
             jax.ShapeDtypeStruct((PEERS, CHUNK + 8, HD), BF16),
         ],
         scratch_shapes=[pltpu.VMEM((KEYS, GW), BF16), pltpu.VMEM((KEYS, GW), BF16)],
+        input_output_aliases={8: 0, 9: 1} if results else {},
         compiler_params=params(),
-        cost_estimate=cost(6),
+        cost_estimate=cost(6 * count / KVH),
         name="grads",
-    )(length, q, g, prefix, prefix, kv_bias, own_kv, own_kv)
+    )(length, q, g, prefix, prefix, kv_bias, own_kv, own_kv, *results)
 
 
 def enclose(pre, parts):
@@ -369,8 +393,9 @@
     q, g, own_kv, e, dp, stat = own(lengths, in_hbm(query[0]), in_hbm(out_grad[0]), in_hbm(resp_kv[0]), query_bias, kv_bias)
     bias = score(q, g, prefix, kv_bias, own_kv, in_hbm(e), in_hbm(dp), stat)
     part = jnp.sum(exchange(bias, PLANE), 0)
-    part, lengths = lax.optimization_barrier((part, lengths))
-    att, dq, own_grad, pre = grads(lengths, q, g, prefix, kv_bias, own_kv)
+    results = grads(0, FIRST, lengths, q, g, prefix, kv_bias, own_kv)
+    part, lengths, results = lax.optimization_barrier((part, lengths, results))
+    att, dq, own_grad, pre = grads(FIRST, KVH - FIRST, lengths, q, g, prefix, kv_bias, own_kv, *results)
     order = [(i + 20) % 32 for i in range(32)]
     part = lax.all_to_all(
         jnp.broadcast_to(part, (32, 2, HD)), COLUMN, 0, 0, axis_index_groups=[order], tiled=True

time: 96 us -> 98.4 us (1.025)
  blocking collectives: 28.4 us -> 17.9 us
  waiting for transfers between devices: 6.04 us -> 12.4 us
  starting transfers between devices: 38.9 us -> 43.8 us
  Pallas kernels: 18.5 us -> 20.1 us
    all_to_all x2 -> x1, blocking collectives: 28.4 us -> 17.9 us  [exchange(): return lax.all_to_all(pieces, axes, 0, 0, tiled=True)]
    all_to_all x1 -> x2, starting transfers between devices: 17.5 us -> 22.4 us  [exchange(): return lax.all_to_all(pieces, axes, 0, 0, tiled=True)]
    all_to_all x1, waiting for transfers between devices: 0.37 us -> 3.57 us  [local(): lax.all_to_all(jnp.broadcast_to(part, (32, 2, HD)), COLUMN, 0, 0, axis_in...]
    all_to_all x1 -> x2, waiting for transfers between devices: 5.67 us -> 8.82 us  [exchange(): return lax.all_to_all(pieces, axes, 0, 0, tiled=True)]
    pallas_call x1 -> x2, Pallas kernels: 7.36 us -> 8.15 us  [grads(): pl.pallas_call(functools.partial(grad_kernel, base), grid=(count,), in_sp...]
  transfers between devices with their start and end apart: 2 -> 3, of which waited for: 2 -> 3; matrix products, arithmetic and copies ran while one was open for 0% -> 0% of each run, Pallas kernels for 13% -> 13%
where the time goes in v3:
time: 98.4 us; the launch traced here: 97.9 us
  starting transfers between devices  43.8 us (45%)
  Pallas kernels  20.1 us (20%)
  blocking collectives  17.9 us (18%)
  waiting for transfers between devices  12.4 us (13%)
  local copies, waits for them, and re-layouts  2.26 us (2%)
  between operations  1.34 us (1%)
    all_to_all x2, starting transfers between devices, exchange(): return lax.all_to_all(pieces, axes, 0, 0, tiled=True)  22.4 us
    all_to_all x1, starting transfers between devices, local(): lax.all_to_all(jnp.broadcast_to(part, (32, 2, HD)), COLUMN, 0, 0, axis_in...  21.4 us
    all_to_all x1, blocking collectives, exchange(): return lax.all_to_all(pieces, axes, 0, 0, tiled=True)  17.9 us
    all_to_all x2, waiting for transfers between devices, exchange(): return lax.all_to_all(pieces, axes, 0, 0, tiled=True)  8.82 us
    pallas_call x2, Pallas kernels, grads(): pl.pallas_call(functools.partial(grad_kernel, base), grid=(count,), in_sp...  8.15 us
    pallas_call x1, Pallas kernels, score(): pl.pallas_call(score_kernel, grid=(KVH,), in_specs=[wide, wide, pl.BlockS...  6.42 us
    pallas_call x1, Pallas kernels, own(): pl.pallas_call(own_kernel, grid=(KVH,), in_specs=[pl.BlockSpec(memory_spa...  4.77 us
    all_to_all x1, waiting for transfers between devices, local(): lax.all_to_all(jnp.broadcast_to(part, (32, 2, HD)), COLUMN, 0, 0, axis_in...  3.57 us
  transfers between devices with their start and end apart: 3, of which 3 were waited for; matrix products, arithmetic and copies ran while one was open for 0% of the time, Pallas kernels for 13%

profile of v3, /device:TPU:1, one launch (start us, length us, event | category | flops | bytes accessed | tf_op | source)
XLA Modules:
  0.0 97.9 jit_solution(4717648915404856158)
XLA Ops:
  0.6 0.0 copy-start
  0.6 0.0 copy-start.1
  0.7 1.6 %broadcast_in_dim.18 = bf16[16,16,1024]{2,1,0:T(8,128)(2,1)} broadcast(bf16[16,1024]{1,0:T(8,128)(2,1)} %bitcast.26), dimensions={1,2} | broadcast | bytes 557056 | tf_op jit(solution)/shard_map/broadcast_in_dim | solution.py:392
  2.3 17.5 %all-to-all-start = ((bf16[16,16,1024]{2,1,0:T(8,128)(2,1)}), bf16[16,16,1024]{2,1,0:T(8,128)(2,1)S(1)}, u32[]{:S(2)}, u32[]{:S(2)}) async-start(bf16[16,16,1024]{2,1,0:T(8,128)(2,1)} %broadcast_in_dim.18), calls=%async_computation | async-start | bytes 1048576 | tf_op jit(solution)/shard_map/all_to_all | solution.py:386
  20.4 0.0 copy-done
  20.4 0.0 copy-done.1
  20.4 4.8 %own.1 = (bf16[128,2560]{1,0:T(8,128)(2,1)S(1)}, bf16[128,2560]{1,0:T(8,128)(2,1)S(1)}, bf16[128,1024]{1,0:T(8,128)(2,1)S(1)}, f32[128,2560]{1,0:T(8,128)}, f32[...) custom-call(s32[1,1]{1,0:T(1,128)S(6)} %copy.19.len_ref, bf16[128,2560]{1,0:T(8,128)(2,1)} %bitcast.27, ...), custom_call_target="tpu_custom_call" | custom-call | flops 251658240 | bytes 4000000 | tf_op jit(solution)/shard_map/own/pallas_call | solution.py:254
  25.2 5.7 %all-to-all-done = bf16[16,16,1024]{2,1,0:T(8,128)(2,1)S(1)} async-done(((bf16[16,16,1024]{2,1,0:T(8,128)(2,1)}), bf16[16,16,1024]{2,1,0:T(8,128)(2,1)S(1)}, u32[]{:S(2)}, u32[]{:S(2)}) %all-to-all-start) | async-done | bytes 524320 | tf_op jit(solution)/shard_map/all_to_all | solution.py:386
  30.9 6.4 %score.1 = f32[32,2,128]{2,1,0:T(2,128)} custom-call(bf16[128,2560]{1,0:T(8,128)(2,1)S(1)} %get-tuple-element.29.q_ref, bf16[128,2560]{1,0:T(8,128)(2,1)S(1)} %get-tuple-element.30.g_ref, bf16[256,1024]{1,0:T(8,128)(2,1)S(1)} %bitcast.13, bf16[256,1024]{1,0:T(8,128)(2,1)S(1)} %bitcast.14, f32[8,128]{1,0:T(8,128)S(1)} %bitcast.20, ...), custom_call_target="tpu_custom_call" | custom-call | flops 754974720 | bytes 4000000 | tf_op jit(solution)/shard_map/score/pallas_call | solution.py:290
  37.3 4.9 %all-to-all-start.1 = ((f32[32,2,128]{2,1,0:T(2,128)}), f32[32,2,128]{2,1,0:T(2,128)S(1)}, u32[]{:S(2)}, u32[]{:S(2)}) async-start(f32[32,2,128]{2,1,0:T(2,128)} %score.1), calls=%async_computation.1 | async-start | bytes 65536 | tf_op jit(solution)/shard_map/all_to_all | solution.py:386
  42.2 4.0 %grads.2 = (bf16[128,2560]{1,0:T(8,128)(2,1)}, bf16[128,2560]{1,0:T(8,128)(2,1)}, bf16[128,1024]{1,0:T(8,128)(2,1)S(1)}, bf16[16,136,128]{2,1,0:T(8,128)(2,1)S(1)}) custom-call(s32[1,1]{1,0:T(1,128)S(6)} %copy.19.len_ref, bf16[128,2560]{1,0:T(8,128)(2,1)S(1)} %get-tuple-element.29.q_ref, bf16[128,2560]{1,0:T(8,128)(2,1)S(1)} %get-tuple-element.30.g_ref, ...), custom_call_target="tpu_custom_call" | custom-call | flops 754974720 | bytes 4000000 | tf_op jit(solution)/shard_map/grads/pallas_call | solution.py:326
  46.2 3.2 %all-to-all-done.1 = f32[32,2,128]{2,1,0:T(2,128)S(1)} async-done(((f32[32,2,128]{2,1,0:T(2,128)}), f32[32,2,128]{2,1,0:T(2,128)S(1)}, u32[]{:S(2)}, u32[]{:S(2)}) %all-to-all-start.1) | async-done | bytes 32800 | tf_op jit(solution)/shard_map/all_to_all | solution.py:386
  49.4 0.6 broadcast_in_dim.22
  50.0 21.4 %all-to-all-start.2 = ((f32[32,2,128]{2,1,0:T(2,128)}), f32[32,2,128]{2,1,0:T(2,128)S(1)}, u32[]{:S(2)}, u32[]{:S(2)}) async-start(f32[32,2,128]{2,1,0:T(2,128)} %broadcast_in_dim.22), calls=%async_computation.2 | async-start | bytes 65536 | tf_op jit(solution)/shard_map/all_to_all | solution.py:400
  71.4 4.2 %grads.3 = (bf16[128,2560]{1,0:T(8,128)(2,1)}, bf16[128,2560]{1,0:T(8,128)(2,1)}, bf16[128,1024]{1,0:T(8,128)(2,1)}, bf16[16,136,128]{2,1,0:T(8,128)(2,1)S(1)}) custom-call(s32[1,1]{1,0:T(1,128)S(6)} %copy.19.len_ref, bf16[128,2560]{1,0:T(8,128)(2,1)S(1)} %get-tuple-element.29.q_ref, ...), custom_call_target="tpu_custom_call", output_to_operand_aliasing={{0}: (8, {}), {1}: (9, {})} | custom-call | flops 754974720 | bytes 4000000 | tf_op jit(solution)/shard_map/grads/pallas_call | solution.py:326
  75.6 3.6 %all-to-all-done.2.parts_ref = f32[32,2,128]{2,1,0:T(2,128)S(1)} async-done(((f32[32,2,128]{2,1,0:T(2,128)}), f32[32,2,128]{2,1,0:T(2,128)S(1)}, u32[]{:S(2)}, u32[]{:S(2)}) %all-to-all-start.2) | async-done | bytes 32800 | tf_op jit(solution)/shard_map/all_to_all | solution.py:400
  79.2 0.1 enclose.1
  79.2 17.9 %all_to_all.20.arrived_ref = bf16[16,136,128]{2,1,0:T(8,128)(2,1)S(1)} all-to-all(bf16[16,136,128]{2,1,0:T(8,128)(2,1)S(1)} %enclose.1), channel_id=1, replica_groups=mesh['grp_0'=2,'grp_1'=4,'grp_2'=2,'dp_0'=32,'dp_1'=2] {'grp_0','grp_1',..., dimensions={0} | all-to-all | bytes 1114112 | tf_op jit(solution)/shard_map/all_to_all | solution.py:386
  97.2 0.7 finish.1
  (1 shorter events, 0.0 us)
Async XLA Ops:
  0.6 19.8 %copy-start = (f32[1024]{0:T(1024)S(1)}, f32[1024]{0:T(1024)}, u32[]{:S(2)}) copy-start(f32[1024]{0:T(1024)} %param.11) | copy-start | bytes 12292
  0.6 19.8 %copy-start.1 = (f32[2560]{0:T(1024)S(1)}, f32[2560]{0:T(1024)}, u32[]{:S(2)}) copy-start(f32[2560]{0:T(1024)} %param.10) | copy-start | bytes 30724
  2.3 28.6 %all-to-all-start = ((bf16[16,16,1024]{2,1,0:T(8,128)(2,1)}), bf16[16,16,1024]{2,1,0:T(8,128)(2,1)S(1)}, u32[]{:S(2)}, u32[]{:S(2)}) async-start(bf16[16,16,1024]{2,1,0:T(8,128)(2,1)} %broadcast_in_dim.18), calls=%async_computation | async-start | bytes 1048576 | tf_op jit(solution)/shard_map/all_to_all | solution.py:386
  37.3 12.1 %all-to-all-start.1 = ((f32[32,2,128]{2,1,0:T(2,128)}), f32[32,2,128]{2,1,0:T(2,128)S(1)}, u32[]{:S(2)}, u32[]{:S(2)}) async-start(f32[32,2,128]{2,1,0:T(2,128)} %score.1), calls=%async_computation.1 | async-start | bytes 65536 | tf_op jit(solution)/shard_map/all_to_all | solution.py:386
  50.0 29.1 %all-to-all-start.2 = ((f32[32,2,128]{2,1,0:T(2,128)}), f32[32,2,128]{2,1,0:T(2,128)S(1)}, u32[]{:S(2)}, u32[]{:S(2)}) async-start(f32[32,2,128]{2,1,0:T(2,128)} %broadcast_in_dim.22), calls=%async_computation.2 | async-start | bytes 65536 | tf_op jit(solution)/shard_map/all_to_all | solution.py:400

commit v4 on v2

--- a/solution.py
+++ b/solution.py
@@ -371,7 +371,7 @@
     part = jnp.sum(exchange(bias, PLANE), 0)
     part, lengths = lax.optimization_barrier((part, lengths))
     att, dq, own_grad, pre = grads(lengths, q, g, prefix, kv_bias, own_kv)
-    order = [(i + 20) % 32 for i in range(32)]
+    order = [(i + 22) % 32 for i in range(32)]
     part = lax.all_to_all(
         jnp.broadcast_to(part, (32, 2, HD)), COLUMN, 0, 0, axis_index_groups=[order], tiled=True
     )

time: 96 us -> 96 us (level)
  waiting for transfers between devices: 6.04 us -> 7.91 us
  starting transfers between devices: 38.9 us -> 37.1 us
    all_to_all x1, waiting for transfers between devices: 0.37 us -> 2.24 us  [local(): lax.all_to_all(jnp.broadcast_to(part, (32, 2, HD)), COLUMN, 0, 0, axis_in...]
    all_to_all x1, starting transfers between devices: 21.4 us -> 19.6 us  [local(): lax.all_to_all(jnp.broadcast_to(part, (32, 2, HD)), COLUMN, 0, 0, axis_in...]
where the time goes in v4:
time: 96 us; the launch traced here: 95.4 us
  starting transfers between devices  37.1 us (39%)
  blocking collectives  28.3 us (29%)
  Pallas kernels  18.5 us (19%)
  waiting for transfers between devices  7.91 us (8%)
  local copies, waits for them, and re-layouts  2.26 us (2%)
  between operations  1.34 us (1%)
    all_to_all x2, blocking collectives, exchange(): return lax.all_to_all(pieces, axes, 0, 0, tiled=True)  28.3 us
    all_to_all x1, starting transfers between devices, local(): lax.all_to_all(jnp.broadcast_to(part, (32, 2, HD)), COLUMN, 0, 0, axis_in...  19.6 us
    all_to_all x1, starting transfers between devices, exchange(): return lax.all_to_all(pieces, axes, 0, 0, tiled=True)  17.5 us
    pallas_call x1, Pallas kernels, grads(): pl.pallas_call(grad_kernel, grid=(KVH,), in_specs=[pl.BlockSpec(memory_sp...  7.36 us
    all_to_all x1, waiting for transfers between devices, exchange(): return lax.all_to_all(pieces, axes, 0, 0, tiled=True)  5.67 us
    pallas_call x1, Pallas kernels, score(): pl.pallas_call(score_kernel, grid=(KVH,), in_specs=[wide, wide, pl.BlockS...  5.6 us
    pallas_call x1, Pallas kernels, own(): pl.pallas_call(own_kernel, grid=(KVH,), in_specs=[pl.BlockSpec(memory_spa...  4.76 us
    all_to_all x1, waiting for transfers between devices, local(): lax.all_to_all(jnp.broadcast_to(part, (32, 2, HD)), COLUMN, 0, 0, axis_in...  2.24 us
  transfers between devices with their start and end apart: 2, of which 2 were waited for; matrix products, arithmetic and copies ran while one was open for 0% of the time, Pallas kernels for 13%

profile of v4, /device:TPU:1, one launch (start us, length us, event | category | flops | bytes accessed | tf_op | source)
XLA Modules:
  0.0 95.4 jit_solution(12762162257220981370)
XLA Ops:
  0.6 0.0 copy-start
  0.6 0.0 copy-start.1
  0.7 1.6 %broadcast_in_dim.18 = bf16[16,16,1024]{2,1,0:T(8,128)(2,1)} broadcast(bf16[16,1024]{1,0:T(8,128)(2,1)} %bitcast.21), dimensions={1,2} | broadcast | bytes 557056 | tf_op jit(solution)/shard_map/broadcast_in_dim | solution.py:368
  2.3 17.5 %all-to-all-start = ((bf16[16,16,1024]{2,1,0:T(8,128)(2,1)}), bf16[16,16,1024]{2,1,0:T(8,128)(2,1)S(1)}, u32[]{:S(2)}, u32[]{:S(2)}) async-start(bf16[16,16,1024]{2,1,0:T(8,128)(2,1)} %broadcast_in_dim.18), calls=%async_computation | async-start | bytes 1048576 | tf_op jit(solution)/shard_map/all_to_all | solution.py:362
  20.4 0.0 copy-done
  20.4 0.0 copy-done.1
  20.4 4.8 %own.1 = (bf16[128,2560]{1,0:T(8,128)(2,1)S(1)}, bf16[128,2560]{1,0:T(8,128)(2,1)S(1)}, bf16[128,1024]{1,0:T(8,128)(2,1)S(1)}, f32[128,2560]{1,0:T(8,128)}, f32[...) custom-call(s32[1,1]{1,0:T(1,128)S(6)} %copy.15.len_ref, bf16[128,2560]{1,0:T(8,128)(2,1)} %bitcast.22, ...), custom_call_target="tpu_custom_call" | custom-call | flops 251658240 | bytes 4000000 | tf_op jit(solution)/shard_map/own/pallas_call | solution.py:238
  25.2 5.7 %all-to-all-done = bf16[16,16,1024]{2,1,0:T(8,128)(2,1)S(1)} async-done(((bf16[16,16,1024]{2,1,0:T(8,128)(2,1)}), bf16[16,16,1024]{2,1,0:T(8,128)(2,1)S(1)}, u32[]{:S(2)}, u32[]{:S(2)}) %all-to-all-start) | async-done | bytes 524320 | tf_op jit(solution)/shard_map/all_to_all | solution.py:362
  30.9 5.6 %score.1 = f32[32,2,128]{2,1,0:T(2,128)S(1)} custom-call(bf16[128,2560]{1,0:T(8,128)(2,1)S(1)} %get-tuple-element.21.q_ref, bf16[128,2560]{1,0:T(8,128)(2,1)S(1)} %get-tuple-element.22.g_ref, bf16[256,1024]{1,0:T(8,128)(2,1)S(1)} %bitcast.13, bf16[256,1024]{1,0:T(8,128)(2,1)S(1)} %bitcast.14, f32[8,128]{1,0:T(8,128)S(1)} %bitcast.18, ...), custom_call_target="tpu_custom_call" | custom-call | flops 754974720 | bytes 4000000 | tf_op jit(solution)/shard_map/score/pallas_call | solution.py:274
  36.5 11.2 %all_to_all.20 = f32[32,2,128]{2,1,0:T(2,128)S(1)} all-to-all(f32[32,2,128]{2,1,0:T(2,128)S(1)} %score.1), channel_id=1, replica_groups=mesh['grp_0'=2,'grp_1'=4,'grp_2'=2,'dp_0'=32,'dp_1'=2] {'grp_0','grp_1',..., dimensions={0} | all-to-all | bytes 65536 | tf_op jit(solution)/shard_map/all_to_all | solution.py:362
  47.7 0.6 broadcast_in_dim.22
  48.3 19.6 %all-to-all-start.2 = ((f32[32,2,128]{2,1,0:T(2,128)}), f32[32,2,128]{2,1,0:T(2,128)S(1)}, u32[]{:S(2)}, u32[]{:S(2)}) async-start(f32[32,2,128]{2,1,0:T(2,128)} %broadcast_in_dim.22), calls=%async_computation.2 | async-start | bytes 65536 | tf_op jit(solution)/shard_map/all_to_all | solution.py:375
  67.9 7.4 %grads.1 = (bf16[128,2560]{1,0:T(8,128)(2,1)}, bf16[128,2560]{1,0:T(8,128)(2,1)}, bf16[128,1024]{1,0:T(8,128)(2,1)}, bf16[16,136,128]{2,1,0:T(8,128)(2,1)S(1)}) custom-call(s32[1,1]{1,0:T(1,128)S(6)} %copy.15.len_ref, bf16[128,2560]{1,0:T(8,128)(2,1)S(1)} %get-tuple-element.21.q_ref, bf16[128,2560]{1,0:T(8,128)(2,1)S(1)} %get-tuple-element.22.g_ref, ...), custom_call_target="tpu_custom_call" | custom-call | flops 1509949440 | bytes 4000000 | tf_op jit(solution)/shard_map/grads/pallas_call | solution.py:299
  75.3 2.2 %all-to-all-done.2.parts_ref = f32[32,2,128]{2,1,0:T(2,128)S(1)} async-done(((f32[32,2,128]{2,1,0:T(2,128)}), f32[32,2,128]{2,1,0:T(2,128)S(1)}, u32[]{:S(2)}, u32[]{:S(2)}) %all-to-all-start.2) | async-done | bytes 32800 | tf_op jit(solution)/shard_map/all_to_all | solution.py:375
  77.5 0.1 enclose.1
  77.6 17.1 %all_to_all.21.arrived_ref = bf16[16,136,128]{2,1,0:T(8,128)(2,1)S(1)} all-to-all(bf16[16,136,128]{2,1,0:T(8,128)(2,1)S(1)} %enclose.1), channel_id=1, replica_groups=mesh['grp_0'=2,'grp_1'=4,'grp_2'=2,'dp_0'=32,'dp_1'=2] {'grp_0','grp_1',..., dimensions={0} | all-to-all | bytes 1114112 | tf_op jit(solution)/shard_map/all_to_all | solution.py:362
  94.7 0.7 finish.1
  (1 shorter events, 0.0 us)
Async XLA Ops:
  0.6 19.8 %copy-start = (f32[1024]{0:T(1024)S(1)}, f32[1024]{0:T(1024)}, u32[]{:S(2)}) copy-start(f32[1024]{0:T(1024)} %param.11) | copy-start | bytes 12292
  0.6 19.8 %copy-start.1 = (f32[2560]{0:T(1024)S(1)}, f32[2560]{0:T(1024)}, u32[]{:S(2)}) copy-start(f32[2560]{0:T(1024)} %param.10) | copy-start | bytes 30724
  2.3 28.6 %all-to-all-start = ((bf16[16,16,1024]{2,1,0:T(8,128)(2,1)}), bf16[16,16,1024]{2,1,0:T(8,128)(2,1)S(1)}, u32[]{:S(2)}, u32[]{:S(2)}) async-start(bf16[16,16,1024]{2,1,0:T(8,128)(2,1)} %broadcast_in_dim.18), calls=%async_computation | async-start | bytes 1048576 | tf_op jit(solution)/shard_map/all_to_all | solution.py:362
  48.3 29.2 %all-to-all-start.2 = ((f32[32,2,128]{2,1,0:T(2,128)}), f32[32,2,128]{2,1,0:T(2,128)S(1)}, u32[]{:S(2)}, u32[]{:S(2)}) async-start(f32[32,2,128]{2,1,0:T(2,128)} %broadcast_in_dim.22), calls=%async_computation.2 | async-start | bytes 65536 | tf_op jit(solution)/shard_map/all_to_all | solution.py:375
